TPU v7x, 32 devices: a whole 2x2x4 slice. The times are simulated.
32 devices in a mesh: sub: 16 (over z, y, x), crs: 2 (over core).
Axes of the slice: x: 2, y: 2, z: 4, core: 2. Of those that a mesh axis runs over, the one named last changes fastest.
Arguments:
- multipliers: float32 [16, 128, 512], P(None, ('sub', 'crs')), may hold values from -6 to 6
- own_modes: float32 [6, 128, 512], P(None, ('sub', 'crs')), may hold values from -0.75 to 0.75
- neighbour_modes: float32 [6, 128, 512], P(None, ('sub', 'crs')), may hold values from -0.75 to 0.75
- face_index: int32 [128, 512], P(('sub', 'crs')), may hold values from 0 to 5, as said below
- neighbour_list: int32 [128, 6], replicated, may hold values from 0 to 127, as said below
- coarse_factor: float32 [768, 768], P('sub', 'crs'), may hold values from -0.21875 to 0.21875
Outputs:
- projected: float32 [16, 128, 512], P(None, ('sub', 'crs'))
Inputs may be any that keep to these rules, and one draw needn't show every extreme that they name: `face_index`: the multipliers of each subdomain lie in 6 contiguous nonempty blocks, face 0 first and face 5 last. `neighbour_list`: subdomain s = (8 x + y) * 8 + z sits at (x, y, z) of a periodic grid of 2 x 8 x 8 subdomains; the 6 faces of each subdomain name its grid neighbours x plus 1, x minus 1, y plus or minus 1, z plus or minus 1 (periodic; along the first dimension both name the same subdomain), in an order that differs from subdomain to subdomain.
All inputs are finite; a program needn't handle non-finite values.
Results may differ from a plain program's by a relative error of at most 0.0001.
Values sent between devices are 32-bit elements; how exact they have to be, the bound alone decides.
A program may use at most 64 MiB of HBM per device.

v0:
```python
import jax
import jax.numpy as jnp
from jax import lax
from jax.sharding import PartitionSpec as P

MODES = 6
NFACE = 6
HIGHEST = lax.Precision.HIGHEST


def shifted(value, axis, by):
    peers = lax.axis_size(axis)
    return lax.ppermute(value, axis, [(i, (i + by) % peers) for i in range(peers)])


def select_columns(portion, positions, wanted):
    matches = (positions[:, None] == wanted[None, :]).astype(jnp.float32)
    return jnp.einsum("krn,nt->krt", portion, matches, precision=HIGHEST)


def body(multipliers, own_modes, neighbour_modes, face_index, neighbour_list, coarse_factor):
    width_rhs = multipliers.shape[0]
    local_subs = multipliers.shape[1]
    crs_size = lax.axis_size("crs")
    sub_size = lax.axis_size("sub")
    crs_rank = lax.axis_index("crs")
    sub_rank = lax.axis_index("sub")
    group_subs = local_subs * crs_size
    faces_dev = local_subs * NFACE
    first_sub = (sub_rank * crs_size + crs_rank) * local_subs
    flat_targets = neighbour_list.reshape(-1)
    row_len = sub_size // 2
    col_len = sub_size // row_len
    row_place = sub_rank % row_len
    local_ids = first_sub + lax.iota(jnp.int32, local_subs)
    first = local_ids // (row_len * group_subs)
    second = local_ids // group_subs % row_len
    third = local_ids % group_subs

    def place(a, b, c):
        return (a * row_len + b) * group_subs + c

    grid_next = jnp.stack(
        [
            place((first + 1) % col_len, second, third),
            place((first + col_len - 1) % col_len, second, third),
            place(first, (second + 1) % row_len, third),
            place(first, (second + row_len - 1) % row_len, third),
            place(first, second, (third + 1) % group_subs),
            place(first, second, (third + group_subs - 1) % group_subs),
        ],
        axis=1,
    )
    local_nbrs = lax.dynamic_slice_in_dim(neighbour_list, first_sub, local_subs, 0)
    matches = (local_nbrs[:, :, None] == grid_next[:, None, :]).astype(jnp.int32)
    first_hit = matches * (jnp.cumsum(matches, axis=2) == 1).astype(jnp.int32)
    face_dir = first_hit.astype(jnp.float32)
    masked_modes = []
    for which_face in range(NFACE):
        masked_modes.append(neighbour_modes * (face_index == which_face).astype(jnp.float32)[None])
    own_coarse = jnp.einsum("ksm,rsm->krs", own_modes, multipliers, precision=HIGHEST)
    face_parts = []
    for which_face in range(NFACE):
        face_parts.append(
            jnp.einsum("ksm,rsm->krs", masked_modes[which_face], multipliers, precision=HIGHEST)
        )
    face_stack = jnp.stack(face_parts, axis=3)
    outgoing = jnp.einsum("krjf,jfd->dkrj", face_stack, face_dir, precision=HIGHEST)
    plans = [(0, row_len), (1, -row_len), (2, 1), (2, 1 - row_len), (3, -1), (3, row_len - 1)]
    arrived = []
    for direction, step in plans:
        arrived.append(shifted(outgoing[direction], "sub", step))
    plus_y = jnp.where(row_place == 0, arrived[3], arrived[2])
    minus_y = jnp.where(row_place == row_len - 1, arrived[5], arrived[4])
    upward = outgoing[4]
    downward = outgoing[5]
    crossing = []
    for piece, step in ((upward[:, :, -1:], 1), (downward[:, :, :1], -1)):
        crossing.append(shifted(piece, "crs", step))
    from_below = jnp.concatenate([crossing[0], upward[:, :, :-1]], axis=2)
    from_above = jnp.concatenate([downward[:, :, 1:], crossing[1]], axis=2)
    own_total = own_coarse + arrived[0] + arrived[1] + plus_y + minus_y + from_below + from_above
    group_coarse = lax.all_gather(own_total, "crs", axis=2, tiled=True)
    coarse_rhs = group_coarse.transpose(2, 0, 1).reshape(group_subs * MODES, width_rhs)
    partial_rows = jnp.einsum("cp,cr->pr", coarse_factor, coarse_rhs, precision=HIGHEST)
    panel_rows = lax.psum(partial_rows, "sub")
    partial_modes = jnp.dot(
        coarse_factor, panel_rows, precision=HIGHEST, preferred_element_type=jnp.float32
    )
    partial_modes = partial_modes.reshape(group_subs, MODES, width_rhs).transpose(1, 2, 0)
    local_targets = lax.dynamic_slice_in_dim(flat_targets, first_sub * NFACE, faces_dev)
    group_amps = lax.psum(partial_modes, "crs")
    own_amps = lax.dynamic_slice_in_dim(group_amps, crs_rank * local_subs, local_subs, 2)
    portion = lax.all_gather(group_amps, "sub", axis=2, tiled=True)
    positions = lax.iota(jnp.int32, portion.shape[2])
    near_amps = select_columns(portion, positions, local_targets)
    near_amps = near_amps.reshape(MODES, width_rhs, local_subs, NFACE)
    applied = jnp.einsum("ksm,krs->rsm", own_modes, own_amps, precision=HIGHEST)
    for which_face in range(NFACE):
        applied = applied + jnp.einsum(
            "ksm,krs->rsm",
            masked_modes[which_face],
            near_amps[:, :, :, which_face],
            precision=HIGHEST,
        )
    return multipliers - applied


def solution(mesh):
    placed = (
        P(None, ("sub", "crs"), None),
        P(None, ("sub", "crs"), None),
        P(None, ("sub", "crs"), None),
        P(("sub", "crs"), None),
        P(),
        P("sub", "crs"),
    )
    return jax.shard_map(
        body, mesh=mesh, in_specs=placed, out_specs=P(None, ("sub", "crs"), None), check_vma=False
    )
```

profile of v0, /device:TPU:0, one launch (start us, length us, event | category | flops | bytes accessed | tf_op | source)
XLA Modules:
  0.0 146.9 jit_solution(12411067293623808287)
XLA Ops:
  0.1 0.6 copy-done.5
  0.8 0.7 copy-done.4
  1.9 0.8 copy-done.3
  2.7 0.9 copy-done.1
  5.7 4.1 %collective-permute-start = (f32[6,16,4]{1,0,2:T(8,128)S(1)}, f32[6,16,4]{1,0,2:T(8,128)S(1)}, u32[]{:S(2)}, u32[]{:S(2)}) collective-permute-start(f32[6,16,4]{1,0,2:T(8,128)S(1)} %get-tuple-element.16), channel_id=1, source_target_pairs={{0,16},{2,18},{4,20},{6,22},{8,24},{10,26},{12,28},{14,30},{16,0},... | collective-permute-start | bytes 4616 | tf_op jit(solution)/shard_map/ppermute | solution.py:13
  9.9 1.3 collective-permute-start.2
  11.1 0.5 collective-permute-start.7
  11.6 1.5 %collective-permute-start.3 = (f32[6,16,4]{1,0,2:T(8,128)S(1)}, f32[6,16,4]{1,0,2:T(8,128)S(1)}, u32[]{:S(2)}, u32[]{:S(2)}) collective-permute-start(f32[6,16,4]{1,0,2:T(8,128)S(1)} %get-tuple-element.11), channel_id=1, source_target_pairs={{0,2},{2,4},{4,6},{6,8},{8,10},{10,12},{12,14},{14,16},{16,18},{18... | collective-permute-start | bytes 4616 | tf_op jit(solution)/shard_map/ppermute | solution.py:13
  13.1 2.7 %collective-permute-start.1 = (f32[6,16,4]{1,0,2:T(8,128)S(1)}, f32[6,16,4]{1,0,2:T(8,128)S(1)}, u32[]{:S(2)}, u32[]{:S(2)}) collective-permute-start(f32[6,16,4]{1,0,2:T(8,128)S(1)} %get-tuple-element.15), channel_id=1, source_target_pairs={{0,16},{2,18},{4,20},{6,22},{8,24},{10,26},{12,28},{14,30},{16,0},... | collective-permute-start | bytes 4616 | tf_op jit(solution)/shard_map/ppermute | solution.py:13
  15.8 2.1 %collective-permute-start.4 = (f32[6,16,4]{1,0,2:T(8,128)S(1)}, f32[6,16,4]{1,0,2:T(8,128)S(1)}, u32[]{:S(2)}, u32[]{:S(2)}) collective-permute-start(f32[6,16,4]{1,0,2:T(8,128)S(1)} %get-tuple-element.14), channel_id=1, source_target_pairs={{0,14},{2,16},{4,18},{6,20},{8,22},{10,24},{12,26},{14,28},{16,30}... | collective-permute-start | bytes 4616 | tf_op jit(solution)/shard_map/ppermute | solution.py:13
  17.9 2.8 %collective-permute-start.5 = (f32[6,16,4]{1,0,2:T(8,128)S(1)}, f32[6,16,4]{1,0,2:T(8,128)S(1)}, u32[]{:S(2)}, u32[]{:S(2)}) collective-permute-start(f32[6,16,4]{1,0,2:T(8,128)S(1)} %get-tuple-element.14), channel_id=1, source_target_pairs={{0,30},{2,0},{4,2},{6,4},{8,6},{10,8},{12,10},{14,12},{16,14},{18,... | collective-permute-start | bytes 4616 | tf_op jit(solution)/shard_map/ppermute | solution.py:13
  21.3 0.8 collective-permute-done.5
  22.4 1.8 %all_gather.6 = f32[6,16,8]{1,0,2:T(8,128)S(1)} all-gather(f32[6,16,4]{1,0,2:T(8,128)S(1)} %fusion.13), channel_id=1, replica_groups=mesh['sub'=16,'crs'=2] {'crs'}, dimensions={2}, use_global_device_ids=true | all-gather | bytes 4608 | tf_op jit(solution)/shard_map/all_gather | solution.py:83
  24.5 77.5 %psum.14 = f32[384,16]{0,1:T(8,128)S(1)} all-reduce(f32[384,16]{0,1:T(8,128)S(1)} %convolution_bitcast_fusion), channel_id=1, replica_groups=mesh['sub'=16,'crs'=2] {'sub'}, use_global_device_ids=true, to_apply=%region_1.2 | all-reduce | flops 6144 | bytes 49152 | tf_op jit(solution)/shard_map/psum | solution.py:86
  102.3 3.4 %psum.15 = f32[6,16,8]{1,0,2:T(8,128)S(1)} all-reduce(f32[6,16,8]{1,0,2:T(8,128)S(1)} %bitcast.135), channel_id=1, replica_groups=mesh['sub'=16,'crs'=2] {'crs'}, use_global_device_ids=true, to_apply=%region_2.3 | all-reduce | flops 768 | bytes 6144 | tf_op jit(solution)/shard_map/psum | solution.py:92
  105.7 37.6 %all_gather.7 = f32[6,16,128]{1,2,0:T(8,128)S(1)} all-gather(f32[6,16,8]{1,2,0:T(8,128)S(1)} %copy.96), channel_id=1, replica_groups=mesh['sub'=16,'crs'=2] {'sub'}, dimensions={2}, use_global_device_ids=true | all-gather | bytes 52224 | tf_op jit(solution)/shard_map/all_gather | solution.py:94
  143.6 0.4 fusion.35
  144.0 0.4 convolution_add_fusion.5
  144.3 0.4 convolution_add_fusion.4
  144.7 0.4 convolution_add_fusion.3
  145.0 0.4 convolution_add_fusion.2
  145.4 0.4 convolution_add_fusion.1
  145.8 0.4 fusion.1
  146.1 0.7 copy.112
  (58 shorter events, 4.4 us)
Async XLA Ops:
  0.0 24.3 %copy-start = (f32[48,384]{1,0:T(8,128)S(1)}, f32[48,384]{1,0:T(8,128)}, u32[]{:S(2)}) copy-start(f32[48,384]{1,0:T(8,128)} %param.11) | copy-start | bytes 221188
  0.0 0.7 copy-start.5
  0.7 0.7 copy-start.4
  1.8 0.8 copy-start.3
  2.6 0.9 copy-start.1
  5.7 12.2 %collective-permute-start = (f32[6,16,4]{1,0,2:T(8,128)S(1)}, f32[6,16,4]{1,0,2:T(8,128)S(1)}, u32[]{:S(2)}, u32[]{:S(2)}) collective-permute-start(f32[6,16,4]{1,0,2:T(8,128)S(1)} %get-tuple-element.16), channel_id=1, source_target_pairs={{0,16},{2,18},{4,20},{6,22},{8,24},{10,26},{12,28},{14,30},{16,0},... | collective-permute-start | bytes 4616 | tf_op jit(solution)/shard_map/ppermute | solution.py:13
  9.9 11.2 %collective-permute-start.2 = (f32[6,16,4]{1,0,2:T(8,128)S(1)}, f32[6,16,4]{1,0,2:T(8,128)S(1)}, u32[]{:S(2)}, u32[]{:S(2)}) collective-permute-start(f32[6,16,4]{1,0,2:T(8,128)S(1)} %get-tuple-element.11), channel_id=1, source_target_pairs={{0,18},{2,20},{4,22},{6,24},{8,26},{10,28},{12,30},{14,0},{16,2},{... | collective-permute-start | bytes 4616 | tf_op jit(solution)/shard_map/ppermute | solution.py:13
  11.1 2.0 %collective-permute-start.6 = (f32[6,16,1]{1,0,2:T(8,128)S(1)}, f32[6,16,1]{1,0,2:T(8,128)S(1)}, u32[]{:S(2)}, u32[]{:S(2)}) collective-permute-start(f32[6,16,1]{1,0,2:T(8,128)S(1)} %slice.71), channel_id=1, source_target_pairs={{0,1},{1,0},{2,3},{3,2},{4,5},{5,4},{6,7},{7,6},{8,9},{9,8},{10,11... | collective-permute-start | bytes 1160 | tf_op jit(solution)/shard_map/ppermute | solution.py:13
  11.1 4.7 %collective-permute-start.7 = (f32[6,16,1]{1,0,2:T(8,128)S(1)}, f32[6,16,1]{1,0,2:T(8,128)S(1)}, u32[]{:S(2)}, u32[]{:S(2)}) collective-permute-start(f32[6,16,1]{1,0,2:T(8,128)S(1)} %slice.75), channel_id=1, source_target_pairs={{0,1},{1,0},{2,3},{3,2},{4,5},{5,4},{6,7},{7,6},{8,9},{9,8},{10,11... | collective-permute-start | bytes 1160 | tf_op jit(solution)/shard_map/ppermute | solution.py:13
  11.6 9.4 %collective-permute-start.3 = (f32[6,16,4]{1,0,2:T(8,128)S(1)}, f32[6,16,4]{1,0,2:T(8,128)S(1)}, u32[]{:S(2)}, u32[]{:S(2)}) collective-permute-start(f32[6,16,4]{1,0,2:T(8,128)S(1)} %get-tuple-element.11), channel_id=1, source_target_pairs={{0,2},{2,4},{4,6},{6,8},{8,10},{10,12},{12,14},{14,16},{16,18},{18... | collective-permute-start | bytes 4616 | tf_op jit(solution)/shard_map/ppermute | solution.py:13
  13.1 7.9 %collective-permute-start.1 = (f32[6,16,4]{1,0,2:T(8,128)S(1)}, f32[6,16,4]{1,0,2:T(8,128)S(1)}, u32[]{:S(2)}, u32[]{:S(2)}) collective-permute-start(f32[6,16,4]{1,0,2:T(8,128)S(1)} %get-tuple-element.15), channel_id=1, source_target_pairs={{0,16},{2,18},{4,20},{6,22},{8,24},{10,26},{12,28},{14,30},{16,0},... | collective-permute-start | bytes 4616 | tf_op jit(solution)/shard_map/ppermute | solution.py:13
  15.8 5.5 %collective-permute-start.4 = (f32[6,16,4]{1,0,2:T(8,128)S(1)}, f32[6,16,4]{1,0,2:T(8,128)S(1)}, u32[]{:S(2)}, u32[]{:S(2)}) collective-permute-start(f32[6,16,4]{1,0,2:T(8,128)S(1)} %get-tuple-element.14), channel_id=1, source_target_pairs={{0,14},{2,16},{4,18},{6,20},{8,22},{10,24},{12,26},{14,28},{16,30}... | collective-permute-start | bytes 4616 | tf_op jit(solution)/shard_map/ppermute | solution.py:13
  17.9 4.2 %collective-permute-start.5 = (f32[6,16,4]{1,0,2:T(8,128)S(1)}, f32[6,16,4]{1,0,2:T(8,128)S(1)}, u32[]{:S(2)}, u32[]{:S(2)}) collective-permute-start(f32[6,16,4]{1,0,2:T(8,128)S(1)} %get-tuple-element.14), channel_id=1, source_target_pairs={{0,30},{2,0},{4,2},{6,4},{8,6},{10,8},{12,10},{14,12},{16,14},{18,... | collective-permute-start | bytes 4616 | tf_op jit(solution)/shard_map/ppermute | solution.py:13
  20.8 1.3 copy-start.2
where the time goes:
time: 147 us
  blocking collectives  120 us (82%)
  starting transfers between devices  14.9 us (10%)
  matrix products  5.56 us (4%)
  local copies, waits for them, and re-layouts  4.53 us (3%)
    psum x1, blocking collectives, body(): panel_rows = lax.psum(partial_rows, 'sub')  77.5 us
    all_gather x1, blocking collectives, body(): portion = lax.all_gather(group_amps, 'sub', axis=2, tiled=True)  37.6 us
    ppermute x8, starting transfers between devices, shifted(): lax.ppermute(value, axis, [(i, (i + by) % peers) for i in range(peers)])  14.9 us
    psum x1, blocking collectives, body(): group_amps = lax.psum(partial_modes, 'crs')  3.41 us
    unnamed x19, local copies, waits for them, and re-layouts  3.1 us
  transfers between devices with their start and end apart: 8, of which 2 were waited for; matrix products, arithmetic and copies ran while one was open for 0% of the time, Pallas kernels for 0%

commit v1 on v0

--- a/solution.py
+++ b/solution.py
@@ -83,7 +83,7 @@
     group_coarse = lax.all_gather(own_total, "crs", axis=2, tiled=True)
     coarse_rhs = group_coarse.transpose(2, 0, 1).reshape(group_subs * MODES, width_rhs)
     partial_rows = jnp.einsum("cp,cr->pr", coarse_factor, coarse_rhs, precision=HIGHEST)
-    panel_rows = lax.psum(partial_rows, "sub")
+    panel_rows = jnp.sum(lax.all_gather(partial_rows, "sub"), axis=0)
     partial_modes = jnp.dot(
         coarse_factor, panel_rows, precision=HIGHEST, preferred_element_type=jnp.float32
     )

time: 147 us -> 112 us (0.76)
  blocking collectives: 120 us -> 83 us
  waiting for transfers between devices: 1.11 us -> 5.02 us
  starting transfers between devices: 14.9 us -> 12.5 us
    psum x1 -> x0, blocking collectives: 77.5 us -> none  [body(): panel_rows = lax.psum(partial_rows, 'sub')]
    all_gather x0 -> x1, blocking collectives: none -> 40.2 us  [body(): panel_rows = jnp.sum(lax.all_gather(partial_rows, 'sub'), axis=0)]
    ppermute x8, waiting for transfers between devices: 1.11 us -> 5.02 us  [shifted(): lax.ppermute(value, axis, [(i, (i + by) % peers) for i in range(peers)])]
    ppermute x8, starting transfers between devices: 14.9 us -> 12.5 us  [shifted(): lax.ppermute(value, axis, [(i, (i + by) % peers) for i in range(peers)])]
    unnamed x19 -> x20, local copies, waits for them, and re-layouts: 3.1 us -> 3.21 us
where the time goes in v1:
time: 112 us; the launch traced here: 111 us
  blocking collectives  83 us (74%)
  starting transfers between devices  12.5 us (11%)
  matrix products  5.56 us (5%)
  waiting for transfers between devices  5.02 us (4%)
  local copies, waits for them, and re-layouts  4.64 us (4%)
    all_gather x1, blocking collectives, body(): panel_rows = jnp.sum(lax.all_gather(partial_rows, 'sub'), axis=0)  40.2 us
    all_gather x1, blocking collectives, body(): portion = lax.all_gather(group_amps, 'sub', axis=2, tiled=True)  37.6 us
    ppermute x8, starting transfers between devices, shifted(): lax.ppermute(value, axis, [(i, (i + by) % peers) for i in range(peers)])  12.5 us
    ppermute x8, waiting for transfers between devices, shifted(): lax.ppermute(value, axis, [(i, (i + by) % peers) for i in range(peers)])  5.02 us
    psum x1, blocking collectives, body(): group_amps = lax.psum(partial_modes, 'crs')  3.41 us
    unnamed x20, local copies, waits for them, and re-layouts  3.21 us
  transfers between devices with their start and end apart: 8, of which 2 were waited for; matrix products, arithmetic and copies ran while one was open for 0% of the time, Pallas kernels for 0%

profile of v1, /device:TPU:0, one launch (start us, length us, event | category | flops | bytes accessed | tf_op | source)
XLA Modules:
  0.0 111.2 jit_solution(5446866513949624800)
XLA Ops:
  0.1 0.7 copy-done.4
  1.1 0.7 copy-done.5
  1.9 0.8 copy-done.3
  2.7 0.9 copy-done.1
  5.7 4.1 %collective-permute-start.1 = (f32[6,16,4]{1,0,2:T(8,128)S(1)}, f32[6,16,4]{1,0,2:T(8,128)S(1)}, u32[]{:S(2)}, u32[]{:S(2)}) collective-permute-start(f32[6,16,4]{1,0,2:T(8,128)S(1)} %get-tuple-element.15), channel_id=1, source_target_pairs={{0,16},{2,18},{4,20},{6,22},{8,24},{10,26},{12,28},{14,30},{16,0},... | collective-permute-start | bytes 4616 | tf_op jit(solution)/shard_map/ppermute | solution.py:13
  9.9 0.5 collective-permute-start.7
  10.4 1.5 %collective-permute-start.3 = (f32[6,16,4]{1,0,2:T(8,128)S(1)}, f32[6,16,4]{1,0,2:T(8,128)S(1)}, u32[]{:S(2)}, u32[]{:S(2)}) collective-permute-start(f32[6,16,4]{1,0,2:T(8,128)S(1)} %get-tuple-element.11), channel_id=1, source_target_pairs={{0,2},{2,4},{4,6},{6,8},{8,10},{10,12},{12,14},{14,16},{16,18},{18... | collective-permute-start | bytes 4616 | tf_op jit(solution)/shard_map/ppermute | solution.py:13
  11.9 1.3 %collective-permute-start.2 = (f32[6,16,4]{1,0,2:T(8,128)S(1)}, f32[6,16,4]{1,0,2:T(8,128)S(1)}, u32[]{:S(2)}, u32[]{:S(2)}) collective-permute-start(f32[6,16,4]{1,0,2:T(8,128)S(1)} %get-tuple-element.11), channel_id=1, source_target_pairs={{0,18},{2,20},{4,22},{6,24},{8,26},{10,28},{12,30},{14,0},{16,2},{... | collective-permute-start | bytes 4616 | tf_op jit(solution)/shard_map/ppermute | solution.py:13
  13.1 2.6 %collective-permute-start = (f32[6,16,4]{1,0,2:T(8,128)S(1)}, f32[6,16,4]{1,0,2:T(8,128)S(1)}, u32[]{:S(2)}, u32[]{:S(2)}) collective-permute-start(f32[6,16,4]{1,0,2:T(8,128)S(1)} %get-tuple-element.16), channel_id=1, source_target_pairs={{0,16},{2,18},{4,20},{6,22},{8,24},{10,26},{12,28},{14,30},{16,0},... | collective-permute-start | bytes 4616 | tf_op jit(solution)/shard_map/ppermute | solution.py:13
  15.7 2.3 %collective-permute-start.5 = (f32[6,16,4]{1,0,2:T(8,128)S(1)}, f32[6,16,4]{1,0,2:T(8,128)S(1)}, u32[]{:S(2)}, u32[]{:S(2)}) collective-permute-start(f32[6,16,4]{1,0,2:T(8,128)S(1)} %get-tuple-element.14), channel_id=1, source_target_pairs={{0,30},{2,0},{4,2},{6,4},{8,6},{10,8},{12,10},{14,12},{16,14},{18,... | collective-permute-start | bytes 4616 | tf_op jit(solution)/shard_map/ppermute | solution.py:13
  18.6 0.9 collective-permute-done.5
  19.5 4.1 %collective-permute-done.4 = f32[6,16,4]{1,0,2:T(8,128)S(1)} collective-permute-done((f32[6,16,4]{1,0,2:T(8,128)S(1)}, f32[6,16,4]{1,0,2:T(8,128)S(1)}, u32[]{:S(2)}, u32[]{:S(2)}) %collective-permute-start.4) | collective-permute-done | bytes 1568 | tf_op jit(solution)/shard_map/ppermute | solution.py:13
  23.9 1.8 %all_gather.12 = f32[6,16,8]{1,0,2:T(8,128)S(1)} all-gather(f32[6,16,4]{1,0,2:T(8,128)S(1)} %fusion.13), channel_id=1, replica_groups=mesh['sub'=16,'crs'=2] {'crs'}, dimensions={2}, use_global_device_ids=true | all-gather | bytes 4608 | tf_op jit(solution)/shard_map/all_gather | solution.py:83
  26.0 40.2 %all-gather = f32[6144,16]{0,1:T(8,128)S(1)} all-gather(f32[384,16]{0,1:T(8,128)S(1)} %convolution_bitcast_fusion), channel_id=2, replica_groups=mesh['sub'=16,'crs'=2] {'sub'}, dimensions={0}, use_global_device_ids=true | all-gather | bytes 417792 | tf_op jit(solution)/shard_map/all_gather | solution.py:86
  66.6 3.4 %psum.7 = f32[6,16,8]{1,0,2:T(8,128)S(1)} all-reduce(f32[6,16,8]{1,0,2:T(8,128)S(1)} %bitcast.141), channel_id=1, replica_groups=mesh['sub'=16,'crs'=2] {'crs'}, use_global_device_ids=true, to_apply=%region_2.3 | all-reduce | flops 768 | bytes 6144 | tf_op jit(solution)/shard_map/psum | solution.py:92
  70.0 0.4 fusion.35
  70.4 37.6 %all_gather.15 = f32[6,16,128]{1,2,0:T(8,128)S(1)} all-gather(f32[6,16,8]{1,2,0:T(8,128)S(1)} %copy.96), channel_id=1, replica_groups=mesh['sub'=16,'crs'=2] {'sub'}, dimensions={2}, use_global_device_ids=true | all-gather | bytes 52224 | tf_op jit(solution)/shard_map/all_gather | solution.py:94
  108.3 0.4 convolution_add_fusion.5
  108.7 0.4 convolution_add_fusion.4
  109.0 0.4 convolution_add_fusion.3
  109.4 0.4 convolution_add_fusion.2
  109.8 0.4 convolution_add_fusion.1
  110.1 0.4 fusion.1
  110.5 0.7 copy.112
  (60 shorter events, 4.5 us)
Async XLA Ops:
  0.0 25.8 %copy-start = (f32[48,384]{1,0:T(8,128)S(1)}, f32[48,384]{1,0:T(8,128)}, u32[]{:S(2)}) copy-start(f32[48,384]{1,0:T(8,128)} %param.11) | copy-start | bytes 221188
  0.1 0.7 copy-start.4
  1.1 0.7 copy-start.5
  1.9 0.8 copy-start.3
  2.7 0.9 copy-start.1
  5.7 12.3 %collective-permute-start.1 = (f32[6,16,4]{1,0,2:T(8,128)S(1)}, f32[6,16,4]{1,0,2:T(8,128)S(1)}, u32[]{:S(2)}, u32[]{:S(2)}) collective-permute-start(f32[6,16,4]{1,0,2:T(8,128)S(1)} %get-tuple-element.15), channel_id=1, source_target_pairs={{0,16},{2,18},{4,20},{6,22},{8,24},{10,26},{12,28},{14,30},{16,0},... | collective-permute-start | bytes 4616 | tf_op jit(solution)/shard_map/ppermute | solution.py:13
  9.9 3.3 %collective-permute-start.6 = (f32[6,16,1]{1,0,2:T(8,128)S(1)}, f32[6,16,1]{1,0,2:T(8,128)S(1)}, u32[]{:S(2)}, u32[]{:S(2)}) collective-permute-start(f32[6,16,1]{1,0,2:T(8,128)S(1)} %slice.71), channel_id=1, source_target_pairs={{0,1},{1,0},{2,3},{3,2},{4,5},{5,4},{6,7},{7,6},{8,9},{9,8},{10,11... | collective-permute-start | bytes 1160 | tf_op jit(solution)/shard_map/ppermute | solution.py:13
  9.9 5.9 %collective-permute-start.7 = (f32[6,16,1]{1,0,2:T(8,128)S(1)}, f32[6,16,1]{1,0,2:T(8,128)S(1)}, u32[]{:S(2)}, u32[]{:S(2)}) collective-permute-start(f32[6,16,1]{1,0,2:T(8,128)S(1)} %slice.75), channel_id=1, source_target_pairs={{0,1},{1,0},{2,3},{3,2},{4,5},{5,4},{6,7},{7,6},{8,9},{9,8},{10,11... | collective-permute-start | bytes 1160 | tf_op jit(solution)/shard_map/ppermute | solution.py:13
  10.4 8.2 %collective-permute-start.3 = (f32[6,16,4]{1,0,2:T(8,128)S(1)}, f32[6,16,4]{1,0,2:T(8,128)S(1)}, u32[]{:S(2)}, u32[]{:S(2)}) collective-permute-start(f32[6,16,4]{1,0,2:T(8,128)S(1)} %get-tuple-element.11), channel_id=1, source_target_pairs={{0,2},{2,4},{4,6},{6,8},{8,10},{10,12},{12,14},{14,16},{16,18},{18... | collective-permute-start | bytes 4616 | tf_op jit(solution)/shard_map/ppermute | solution.py:13
  11.9 6.7 %collective-permute-start.2 = (f32[6,16,4]{1,0,2:T(8,128)S(1)}, f32[6,16,4]{1,0,2:T(8,128)S(1)}, u32[]{:S(2)}, u32[]{:S(2)}) collective-permute-start(f32[6,16,4]{1,0,2:T(8,128)S(1)} %get-tuple-element.11), channel_id=1, source_target_pairs={{0,18},{2,20},{4,22},{6,24},{8,26},{10,28},{12,30},{14,0},{16,2},{... | collective-permute-start | bytes 4616 | tf_op jit(solution)/shard_map/ppermute | solution.py:13
  13.1 5.5 %collective-permute-start = (f32[6,16,4]{1,0,2:T(8,128)S(1)}, f32[6,16,4]{1,0,2:T(8,128)S(1)}, u32[]{:S(2)}, u32[]{:S(2)}) collective-permute-start(f32[6,16,4]{1,0,2:T(8,128)S(1)} %get-tuple-element.16), channel_id=1, source_target_pairs={{0,16},{2,18},{4,20},{6,22},{8,24},{10,26},{12,28},{14,30},{16,0},... | collective-permute-start | bytes 4616 | tf_op jit(solution)/shard_map/ppermute | solution.py:13
  15.7 3.8 %collective-permute-start.5 = (f32[6,16,4]{1,0,2:T(8,128)S(1)}, f32[6,16,4]{1,0,2:T(8,128)S(1)}, u32[]{:S(2)}, u32[]{:S(2)}) collective-permute-start(f32[6,16,4]{1,0,2:T(8,128)S(1)} %get-tuple-element.14), channel_id=1, source_target_pairs={{0,30},{2,0},{4,2},{6,4},{8,6},{10,8},{12,10},{14,12},{16,14},{18,... | collective-permute-start | bytes 4616 | tf_op jit(solution)/shard_map/ppermute | solution.py:13
  18.1 5.5 %collective-permute-start.4 = (f32[6,16,4]{1,0,2:T(8,128)S(1)}, f32[6,16,4]{1,0,2:T(8,128)S(1)}, u32[]{:S(2)}, u32[]{:S(2)}) collective-permute-start(f32[6,16,4]{1,0,2:T(8,128)S(1)} %get-tuple-element.14), channel_id=1, source_target_pairs={{0,14},{2,16},{4,18},{6,20},{8,22},{10,24},{12,26},{14,28},{16,30}... | collective-permute-start | bytes 4616 | tf_op jit(solution)/shard_map/ppermute | solution.py:13
  18.4 5.3 %copy-start.2 = (f32[6,4,512]{2,1,0:T(4,128)S(1)}, f32[6,4,512]{2,1,0:T(4,128)}, u32[]{:S(2)}) copy-start(f32[6,4,512]{2,1,0:T(4,128)} %param.7) | copy-start | bytes 147460
